TPU v7x, 32 devices: a whole 2x2x4 slice. The times are simulated.
32 devices in a mesh: fsdp: 2 (over x), ctx: 4 (over y, core), tp: 4 (over z).
Axes of the slice: x: 2, y: 2, z: 4, core: 2. Of those that a mesh axis runs over, the one named last changes fastest.
Arguments:
- tokens: bfloat16 [8, 1024, 2048], P('fsdp', 'ctx'), may hold values from -8 to 8
- positions: int32 [8, 1024], P('fsdp', 'ctx'), may hold values from 0 to 383, as said below
- block_ids: int32 [8, 1024], P('fsdp', 'ctx'), may hold values from 0 to 3, as said below
- gain_attend: bfloat16 [2048], P('fsdp'), may hold values from 0.099609375 to 1.8984375
- w_query: bfloat16 [2048, 2048], P('fsdp', 'tp'), may hold values from -0.125 to 0.125
- w_key: bfloat16 [2048, 2048], P('fsdp', 'tp'), may hold values from -0.125 to 0.125
- w_value: bfloat16 [2048, 2048], P('fsdp', 'tp'), may hold values from -0.125 to 0.125
- w_output: bfloat16 [2048, 2048], P('tp', 'fsdp'), may hold values from -1 to 1
- gain_feed: bfloat16 [2048], P('fsdp'), may hold values from 0.099609375 to 1.8984375
- w_gate: bfloat16 [2048, 8192], P('fsdp', 'tp'), may hold values from -0.125 to 0.125
- w_up: bfloat16 [2048, 8192], P('fsdp', 'tp'), may hold values from -0.125 to 0.125
- w_down: bfloat16 [8192, 2048], P('tp', 'fsdp'), may hold values from -0.0625 to 0.0625
- cotangent: bfloat16 [8, 1024, 2048], P('fsdp', 'ctx'), may hold values from -6 to 6
Outputs:
- layer_out: bfloat16 [8, 1024, 2048], P('fsdp', 'ctx')
- grad_input: bfloat16 [8, 1024, 2048], P('fsdp', 'ctx')
- grad_gain_attend: float32 [2048], P(('fsdp', 'ctx'))
- grad_w_query: float32 [2048, 2048], P(('fsdp', 'ctx'), 'tp')
- grad_w_key: float32 [2048, 2048], P(('fsdp', 'ctx'), 'tp')
- grad_w_value: float32 [2048, 2048], P(('fsdp', 'ctx'), 'tp')
- grad_w_output: float32 [2048, 2048], P('tp', ('fsdp', 'ctx'))
- grad_gain_feed: float32 [2048], P(('fsdp', 'ctx'))
- grad_w_gate: float32 [2048, 8192], P(('fsdp', 'ctx'), 'tp')
- grad_w_up: float32 [2048, 8192], P(('fsdp', 'ctx'), 'tp')
- grad_w_down: float32 [8192, 2048], P('tp', ('fsdp', 'ctx'))
- stream_rms: float32 [], replicated
- attend_rms: float32 [], replicated
- feed_rms: float32 [], replicated
Inputs may be any that keep to these rules, and one draw needn't show every extreme that they name: Along each sequence, positions count 0, 1, 2 and so on from the first token of each block, a run of equal block ids. `block_ids`: along each sequence block ids start at 0, never fall and rise by one at each new block.
All inputs are finite; a program needn't handle non-finite values.
Results may differ from a plain program's by a relative error of at most 0.015.
Values may be sent and summed in bfloat16 or wider, within the bound.
A program may use at most 256 MiB of HBM per device.

v0:
```python
import math
import jax
import jax.numpy as jnp
from jax import lax
from jax.sharding import PartitionSpec as P

HD = 128
norm_epsilon = 1e-05
rope_base = 10000.0


def plain_dot(left_side, right_side):
    return jnp.dot(left_side, right_side, preferred_element_type=jnp.float32)


def dot_last(left_side, right_side):
    return lax.dot_general(
        left_side, right_side, (((1,), (1,)), ((), ())), preferred_element_type=jnp.float32
    )


def dot_first(left_side, right_side):
    return lax.dot_general(
        left_side, right_side, (((0,), (0,)), ((), ())), preferred_element_type=jnp.float32
    )


def inverse_rms(values):
    return lax.rsqrt(jnp.mean(values * values, axis=-1, keepdims=True) + norm_epsilon)


def norm_back(grad_norm, values, scale_rows, gain):
    weighted = grad_norm * gain
    inner_mean = jnp.mean(weighted * values, axis=-1, keepdims=True)
    grad_values = (
        scale_rows * weighted - values * (scale_rows * scale_rows * scale_rows) * inner_mean
    )
    grad_gain = jnp.sum(grad_norm * (values * scale_rows), axis=0)
    return (grad_values, grad_gain)


def rope_tables(positions, head_size):
    half_size = head_size // 2
    inverse = jnp.exp(
        jnp.arange(half_size, dtype=jnp.float32) * (-2.0 * math.log(rope_base) / head_size)
    )
    turned = positions.astype(jnp.float32)[..., None, None] * inverse
    return (jnp.cos(turned), jnp.sin(turned))


def rotate(values, cosine, sine_table, direction):
    half_size = values.shape[-1] // 2
    first_half = values[..., :half_size]
    second_half = values[..., half_size:]
    return jnp.concatenate(
        [
            first_half * cosine - direction * (second_half * sine_table),
            direction * (first_half * sine_table) + second_half * cosine,
        ],
        axis=-1,
    )


def local(
    tokens,
    positions,
    block_ids,
    gain_attend,
    w_query,
    w_key,
    w_value,
    w_output,
    gain_feed,
    w_gate,
    w_up,
    w_down,
    cotangent,
):
    seq_count, block_len, model_width = tokens.shape
    row_count = seq_count * block_len
    seq_len = block_len * lax.axis_size("ctx")
    heads_here = w_query.shape[1] // HD
    score_scale = 1.0 / math.sqrt(HD)
    score_shift = math.log(seq_len)
    shape_heads = (seq_count, block_len, heads_here, HD)
    stream = tokens.reshape(row_count, model_width).astype(jnp.float32)
    query_full, key_full, value_full, output_full, gain_one = (
        lax.all_gather(w_query, "fsdp", axis=0, tiled=True),
        lax.all_gather(w_key, "fsdp", axis=0, tiled=True),
        lax.all_gather(w_value, "fsdp", axis=0, tiled=True),
        lax.all_gather(w_output, "fsdp", axis=1, tiled=True),
        lax.all_gather(gain_attend, "fsdp", axis=0, tiled=True),
    )
    gain_one = gain_one.astype(jnp.float32)
    scale_one = inverse_rms(stream)
    normed_one = (stream * scale_one * gain_one).astype(jnp.bfloat16)
    queries = plain_dot(normed_one, query_full)
    key_proj = plain_dot(normed_one, key_full)
    values = plain_dot(normed_one, value_full).astype(jnp.bfloat16)
    cosine, sine_table = rope_tables(positions, HD)
    query_rot = rotate(queries.reshape(shape_heads), cosine, sine_table, 1.0).astype(jnp.bfloat16)
    key_rot = (
        rotate(key_proj.reshape(shape_heads), cosine, sine_table, 1.0)
        .astype(jnp.bfloat16)
        .reshape(seq_count, block_len, heads_here * HD)
    )
    value_rows = values.reshape(seq_count, block_len, heads_here * HD)
    query_tags = block_ids.astype(jnp.float32)
    key_tags = block_ids.astype(jnp.bfloat16)

    def scores_of(portion):
        key_piece, value_piece, tag_piece = portion
        span = key_piece.shape[1]
        key_heads = key_piece.reshape(seq_count, span, heads_here, HD)
        value_heads = value_piece.reshape(seq_count, span, heads_here, HD)
        logits = (
            jnp.einsum("sqhd,skhd->shqk", query_rot, key_heads, preferred_element_type=jnp.float32)
            * score_scale
            - score_shift
        )
        allowed = tag_piece.astype(jnp.float32)[:, None, None, :] <= query_tags[:, None, :, None]
        return (key_heads, value_heads, jax.nn.sigmoid(logits), allowed)

    key_heads, value_heads, squashed, allowed = scores_of(
        (
            lax.all_gather(key_rot, "ctx", axis=1, tiled=True),
            lax.all_gather(value_rows, "ctx", axis=1, tiled=True),
            lax.all_gather(key_tags, "ctx", axis=1, tiled=True),
        )
    )
    weights = jnp.where(allowed, squashed, 0.0).astype(jnp.bfloat16)
    attended = jnp.einsum(
        "shqk,skhd->sqhd", weights, value_heads, preferred_element_type=jnp.float32
    )
    mixed_rows = attended.reshape(row_count, heads_here * HD).astype(jnp.bfloat16)
    attend_out = lax.psum(plain_dot(mixed_rows, output_full), "tp")
    middle = stream + attend_out
    gate_full, up_full, down_full, gain_two = (
        lax.all_gather(w_gate, "fsdp", axis=0, tiled=True),
        lax.all_gather(w_up, "fsdp", axis=0, tiled=True),
        lax.all_gather(w_down, "fsdp", axis=1, tiled=True),
        lax.all_gather(gain_feed, "fsdp", axis=0, tiled=True),
    )
    gain_two = gain_two.astype(jnp.float32)
    scale_two = inverse_rms(middle)
    normed_two = (middle * scale_two * gain_two).astype(jnp.bfloat16)
    gate_vals = plain_dot(normed_two, gate_full)
    up_vals = plain_dot(normed_two, up_full)
    gate_sig = jax.nn.sigmoid(gate_vals)
    gate_act = gate_vals * gate_sig
    hidden = (gate_act * up_vals).astype(jnp.bfloat16)
    feed_out = lax.psum(plain_dot(hidden, down_full), "tp")
    result = middle + feed_out
    layer_out = result.astype(jnp.bfloat16).reshape(tokens.shape)
    totals = lax.psum(
        (jnp.sum(result * result), jnp.sum(attend_out * attend_out), jnp.sum(feed_out * feed_out)),
        ("fsdp", "ctx"),
    )
    entries = float(row_count * model_width * lax.axis_size("fsdp") * lax.axis_size("ctx"))
    stream_rms = jnp.sqrt(totals[0] / entries)
    attend_rms = jnp.sqrt(totals[1] / entries)
    feed_rms = jnp.sqrt(totals[2] / entries)
    query_full, key_full, value_full, output_full, gate_full, up_full, down_full = (
        lax.all_gather(w_query, "fsdp", axis=0, tiled=True),
        lax.all_gather(w_key, "fsdp", axis=0, tiled=True),
        lax.all_gather(w_value, "fsdp", axis=0, tiled=True),
        lax.all_gather(w_output, "fsdp", axis=1, tiled=True),
        lax.all_gather(w_gate, "fsdp", axis=0, tiled=True),
        lax.all_gather(w_up, "fsdp", axis=0, tiled=True),
        lax.all_gather(w_down, "fsdp", axis=1, tiled=True),
    )
    grad_rows = cotangent.reshape(row_count, model_width)
    grad_stream = grad_rows.astype(jnp.float32)
    grad_hidden = dot_last(grad_rows, down_full)
    grad_down = dot_first(hidden, grad_rows)
    slope = gate_sig * (1.0 + gate_vals * (1.0 - gate_sig))
    grad_gate = (grad_hidden * up_vals * slope).astype(jnp.bfloat16)
    grad_up = (grad_hidden * gate_act).astype(jnp.bfloat16)
    grad_normed_two = lax.psum(dot_last(grad_gate, gate_full) + dot_last(grad_up, up_full), "tp")
    grad_gate_w = dot_first(normed_two, grad_gate)
    grad_up_w = dot_first(normed_two, grad_up)
    grad_middle_norm, grad_gain_two = norm_back(grad_normed_two, middle, scale_two, gain_two)
    grad_middle = grad_stream + grad_middle_norm
    grad_attend = grad_middle.astype(jnp.bfloat16)
    grad_mixed = dot_last(grad_attend, output_full).astype(jnp.bfloat16)
    grad_output_w = dot_first(mixed_rows, grad_attend)
    grad_mixed_heads = grad_mixed.reshape(shape_heads)
    key_heads, value_heads, squashed, allowed = scores_of(
        (
            lax.all_gather(key_rot, "ctx", axis=1, tiled=True),
            lax.all_gather(value_rows, "ctx", axis=1, tiled=True),
            lax.all_gather(key_tags, "ctx", axis=1, tiled=True),
        )
    )
    span = key_heads.shape[1]
    weights = jnp.where(allowed, squashed, 0.0).astype(jnp.bfloat16)
    grad_weights = jnp.einsum(
        "sqhd,skhd->shqk", grad_mixed_heads, value_heads, preferred_element_type=jnp.float32
    )
    grad_logits = jnp.where(allowed, grad_weights * squashed * (1.0 - squashed), 0.0).astype(
        jnp.bfloat16
    )
    grad_query = score_scale * jnp.einsum(
        "shqk,skhd->sqhd", grad_logits, key_heads, preferred_element_type=jnp.float32
    )
    key_part = (
        score_scale
        * jnp.einsum("shqk,sqhd->skhd", grad_logits, query_rot, preferred_element_type=jnp.float32)
    ).reshape(seq_count, span, heads_here * HD)
    value_part = jnp.einsum(
        "shqk,sqhd->skhd", weights, grad_mixed_heads, preferred_element_type=jnp.float32
    ).reshape(seq_count, span, heads_here * HD)
    grad_key_mine, grad_value_mine = (
        lax.psum_scatter(key_part, "ctx", scatter_dimension=1, tiled=True),
        lax.psum_scatter(value_part, "ctx", scatter_dimension=1, tiled=True),
    )
    grad_query_rows = (
        rotate(grad_query, cosine, sine_table, -1.0)
        .reshape(row_count, heads_here * HD)
        .astype(jnp.bfloat16)
    )
    grad_key_rows = (
        rotate(grad_key_mine.reshape(shape_heads), cosine, sine_table, -1.0)
        .reshape(row_count, heads_here * HD)
        .astype(jnp.bfloat16)
    )
    grad_value_rows = grad_value_mine.reshape(row_count, heads_here * HD).astype(jnp.bfloat16)
    grad_normed_one = lax.psum(
        dot_last(grad_query_rows, query_full)
        + dot_last(grad_key_rows, key_full)
        + dot_last(grad_value_rows, value_full),
        "tp",
    )
    grad_query_w = dot_first(normed_one, grad_query_rows)
    grad_key_w = dot_first(normed_one, grad_key_rows)
    grad_value_w = dot_first(normed_one, grad_value_rows)
    grad_input_norm, grad_gain_one = norm_back(grad_normed_one, stream, scale_one, gain_one)
    grad_input = (grad_middle + grad_input_norm).astype(jnp.bfloat16).reshape(tokens.shape)
    summed = (
        lax.psum_scatter(grad_gain_one, ("fsdp", "ctx"), scatter_dimension=0, tiled=True),
        lax.psum_scatter(grad_query_w, ("fsdp", "ctx"), scatter_dimension=0, tiled=True),
        lax.psum_scatter(grad_key_w, ("fsdp", "ctx"), scatter_dimension=0, tiled=True),
        lax.psum_scatter(grad_value_w, ("fsdp", "ctx"), scatter_dimension=0, tiled=True),
        lax.psum_scatter(grad_output_w, ("fsdp", "ctx"), scatter_dimension=1, tiled=True),
        lax.psum_scatter(grad_gain_two, ("fsdp", "ctx"), scatter_dimension=0, tiled=True),
        lax.psum_scatter(grad_gate_w, ("fsdp", "ctx"), scatter_dimension=0, tiled=True),
        lax.psum_scatter(grad_up_w, ("fsdp", "ctx"), scatter_dimension=0, tiled=True),
        lax.psum_scatter(grad_down, ("fsdp", "ctx"), scatter_dimension=1, tiled=True),
    )
    return (
        layer_out,
        grad_input,
        summed[0],
        summed[1],
        summed[2],
        summed[3],
        summed[4],
        summed[5],
        summed[6],
        summed[7],
        summed[8],
        stream_rms,
        attend_rms,
        feed_rms,
    )


def solution(mesh):
    placed = (
        P("fsdp", "ctx", None),
        P("fsdp", "ctx"),
        P("fsdp", "ctx"),
        P("fsdp"),
        P("fsdp", "tp"),
        P("fsdp", "tp"),
        P("fsdp", "tp"),
        P("tp", "fsdp"),
        P("fsdp"),
        P("fsdp", "tp"),
        P("fsdp", "tp"),
        P("tp", "fsdp"),
        P("fsdp", "ctx", None),
    )
    return jax.shard_map(
        local,
        mesh=mesh,
        in_specs=placed,
        out_specs=(
            P("fsdp", "ctx", None),
            P("fsdp", "ctx", None),
            P(("fsdp", "ctx")),
            P(("fsdp", "ctx"), "tp"),
            P(("fsdp", "ctx"), "tp"),
            P(("fsdp", "ctx"), "tp"),
            P("tp", ("fsdp", "ctx")),
            P(("fsdp", "ctx")),
            P(("fsdp", "ctx"), "tp"),
            P(("fsdp", "ctx"), "tp"),
            P("tp", ("fsdp", "ctx")),
            P(),
            P(),
            P(),
        ),
        check_vma=False,
    )
```

profile of v0, /device:TPU:0, one launch (start us, length us, event | category | flops | bytes accessed | tf_op | source)
XLA Modules:
  0.0 2545.2 jit_solution(7070096330234557118)
XLA Ops:
  9.4 5.5 all_gather.46
  14.9 3.1 fusion.4
  18.7 5.6 fusion.6
  25.4 20.0 all-gather.16.cloned.1.call-done
  45.4 2.9 copy.52
  48.3 31.7 %all-gather.14.cloned.1.call-done = bf16[2048,512]{1,0:T(8,128)(2,1)} async-done(((bf16[1024,512]{1,0:T(8,128)(2,1)}), bf16[2048,512]{1,0:T(8,128)(2,1)}) %all-gather.14.cloned.1.call-update) | async-done | bytes 2097168 | tf_op jit(solution)/shard_map/all_gather | solution.py:88
  80.0 3.9 copy.51
  84.0 4.7 fusion.13
  93.1 5.2 fusion.2
  98.3 16.4 all-gather.10.cloned.1.call-done
  114.7 6.2 convolution_convert_fusion
  121.6 5.4 all_gather.49
  127.6 24.1 all-gather.18.cloned.1.call-done
  151.7 11.6 add_divide_fusion
  163.3 24.9 all-gather.12.cloned.1.call-done
  188.2 6.2 copy.50
  194.4 11.0 fusion.27
  206.1 16.6 all-gather.20.cloned.1.call-done
  222.7 7.2 fusion.37
  232.1 4.8 all_gather.54
  236.9 284.1 %all-reduce.8.cloned.1.call-done = f32[1024,2048]{1,0:T(8,128)} async-done(((f32[1024,2048]{1,0:T(8,128)}), f32[1024,2048]{1,0:T(8,128)}) %all-reduce.8.cloned.1.call-update) | async-done | bytes 8388624 | tf_op jit(solution)/shard_map/psum | solution.py:136
  520.9 7.6 multiply_reduce_fusion.5
  528.5 4.3 copy-done
  535.6 89.9 %all-gather.22.cloned.1.call-done = bf16[2048,2048]{1,0:T(8,128)(2,1)} async-done(((bf16[1024,2048]{1,0:T(8,128)(2,1)}), bf16[2048,2048]{1,0:T(8,128)(2,1)}) %all-gather.22.cloned.1.call-update) | async-done | bytes 8388624 | tf_op jit(solution)/shard_map/all_gather | solution.py:139
  625.5 14.6 fusion.51
  640.0 91.0 %all-gather.24.cloned.1.call-done = bf16[2048,2048]{1,0:T(8,128)(2,1)} async-done(((bf16[1024,2048]{1,0:T(8,128)(2,1)}), bf16[2048,2048]{1,0:T(8,128)(2,1)}) %all-gather.24.cloned.1.call-update) | async-done | bytes 8388624 | tf_op jit(solution)/shard_map/all_gather | solution.py:140
  731.0 14.5 fusion.52
  745.5 90.9 %all-gather.26.cloned.1.call-done = bf16[2048,2048]{1,0:T(8,128)(2,1)} async-done(((bf16[2048,1024]{1,0:T(8,128)(2,1)}), bf16[2048,2048]{1,0:T(8,128)(2,1)}) %all-gather.26.cloned.1.call-update) | async-done | bytes 8388624 | tf_op jit(solution)/shard_map/all_gather | solution.py:141
  836.4 21.9 multiply_convert_fusion
  858.3 12.7 fusion.54
  871.1 12.7 fusion.53
  883.8 13.3 convolution_add_fusion
  897.2 562.3 %all-reduce.12.cloned.1.call-done = (f32[1024,2048]{1,0:T(8,128)}, f32[1024,2048]{1,0:T(8,128)}) async-done(((f32[1024,2048]{1,0:T(8,128)}, f32[1024,2048]{1,0:T(8,128)}), (f32[1024,2048]{1,0:T(8,128)}, f32[1024,2048]{1,0:T(8,128)})) %all-reduce.12.cloned.1.call-update) | async-done | bytes 16777232 | tf_op jit(solution)/shard_map/psum | solution.py:152
  1459.6 15.1 multiply_reduce_fusion
  1474.6 4.7 subtract_add_fusion
  1479.4 3.2 copy-done.1
  1482.6 4.0 fusion.23
  1489.3 9.5 select_convert_fusion
  1498.8 6.3 broadcast_multiply_fusion
  1505.2 13.1 fusion.17
  1518.3 9.0 copy.61
  1527.4 7.7 multiply_bitcast_fusion
  1535.1 40.4 %reduce-scatter.10.cloned.1.call-done = f32[4,256,512]{1,2,0:T(8,128)} async-done(((f32[4,1024,512]{1,2,0:T(8,128)}), f32[4,256,512]{1,2,0:T(8,128)}) %reduce-scatter.10.cloned.1.call-update) | async-done | bytes 2097168 | tf_op jit(solution)/shard_map/reduce_scatter | solution.py:214
  1580.6 68.9 %reduce-scatter.12.cloned.1.call-done = f32[4,256,512]{2,1,0:T(8,128)} async-done(((f32[4,1024,512]{2,1,0:T(8,128)}), f32[4,256,512]{2,1,0:T(8,128)}) %reduce-scatter.12.cloned.1.call-update) | async-done | bytes 2097168 | tf_op jit(solution)/shard_map/reduce_scatter | solution.py:215
  1651.3 4.3 fusion.30
  1658.0 5.8 add_add_fusion
  1665.1 7.7 fusion.19
  1672.9 15.6 fusion.55
  1688.5 15.4 fusion.56
  1704.0 15.6 fusion.57
  1719.7 6.6 convolution_bitcast_fusion
  1726.4 6.6 fusion.32
  1733.1 6.5 fusion.28
  1741.0 213.9 %all-reduce.10.cloned.1.call-done = f32[1024,2048]{1,0:T(8,128)} async-done(((f32[1024,2048]{1,0:T(8,128)}), f32[1024,2048]{1,0:T(8,128)}) %all-reduce.10.cloned.1.call-update) | async-done | bytes 8388624 | tf_op jit(solution)/shard_map/psum | solution.py:228
  1954.9 6.4 fusion.3
  1961.3 25.5 %all-reduce.2 = (f32[2048]{0:T(1024)S(1)}, f32[2048]{0:T(1024)S(1)}, f32[]{:T(128)}, f32[]{:T(128)}, f32[]{:T(128)}) all-reduce(f32[2048]{0:T(1024)S(1)} %get-tuple-element.16, f32[2048]{0:T(1024)S(1)} %copy-done.27, f32[]{:T(128)} %get-tuple-element.19, ...), channel_id=4, replica_groups=mesh['fsdp'=2,'ctx'=4,'tp'=4] {'fsdp','ctx'}, use_global_device_ids=true, to_apply=%region_11.12.clone | all-reduce | flops 4099 | bytes 32792
  1990.2 10.5 fusion.10
  2000.6 8.1 reduce-scatter.20.cloned.1.call-done
  2008.8 120.2 %reduce-scatter.22.cloned.1.call-done = f32[256,2048]{1,0:T(8,128)} async-done(((f32[2048,2048]{1,0:T(8,128)}), f32[256,2048]{1,0:T(8,128)}) %reduce-scatter.22.cloned.1.call-update) | async-done | bytes 2097168 | tf_op jit(solution)/shard_map/reduce_scatter | solution.py:246
  2129.0 120.2 %reduce-scatter.24.cloned.1.call-done = f32[256,2048]{1,0:T(8,128)} async-done(((f32[2048,2048]{1,0:T(8,128)}), f32[256,2048]{1,0:T(8,128)}) %reduce-scatter.24.cloned.1.call-update) | async-done | bytes 2097168 | tf_op jit(solution)/shard_map/reduce_scatter | solution.py:247
  2249.2 120.0 %reduce-scatter.26.cloned.1.call-done = f32[2048,256]{1,0:T(8,128)} async-done(((f32[2048,2048]{1,0:T(8,128)}), f32[2048,256]{1,0:T(8,128)}) %reduce-scatter.26.cloned.1.call-update) | async-done | bytes 2097168 | tf_op jit(solution)/shard_map/reduce_scatter | solution.py:248
  2369.2 55.1 %reduce-scatter.18.cloned.1.call-done = f32[256,512]{1,0:T(8,128)} async-done(((f32[2048,512]{1,0:T(8,128)}), f32[256,512]{1,0:T(8,128)}) %reduce-scatter.18.cloned.1.call-update) | async-done | bytes 524304 | tf_op jit(solution)/shard_map/reduce_scatter | solution.py:243
  2424.3 55.0 %reduce-scatter.14.cloned.1.call-done = f32[256,512]{1,0:T(8,128)} async-done(((f32[2048,512]{1,0:T(8,128)}), f32[256,512]{1,0:T(8,128)}) %reduce-scatter.14.cloned.1.call-update) | async-done | bytes 524304 | tf_op jit(solution)/shard_map/reduce_scatter | solution.py:241
  2479.3 55.1 %reduce-scatter.16.cloned.1.call-done = f32[256,512]{1,0:T(8,128)} async-done(((f32[2048,512]{1,0:T(8,128)}), f32[256,512]{1,0:T(8,128)}) %reduce-scatter.16.cloned.1.call-update) | async-done | bytes 524304 | tf_op jit(solution)/shard_map/reduce_scatter | solution.py:242
  (136 shorter events, 30.7 us)
Async XLA Ops:
  7.2 38.2 %all-gather.16.cloned.1.call-start = ((), (), s32[]{:S(2)}) async-start(), calls=%async_computation.12 | async-start | bytes 3145728 | tf_op jit(solution)/shard_map/all_gather | solution.py:89
  7.9 72.1 %all-gather.14.cloned.1.call-start = ((), (), s32[]{:S(2)}) async-start(), calls=%async_computation.11 | async-start | bytes 3145728 | tf_op jit(solution)/shard_map/all_gather | solution.py:88
  8.7 106.1 %all-gather.10.cloned.1.call-start = ((), (), s32[]{:S(2)}) async-start(), calls=%async_computation.9 | async-start | bytes 3145728 | tf_op jit(solution)/shard_map/all_gather | solution.py:90
  9.4 142.3 %all-gather.18.cloned.1.call-start = ((), (), s32[]{:S(2)}) async-start(), calls=%async_computation.13 | async-start | bytes 5242880 | tf_op jit(solution)/shard_map/all_gather | solution.py:126
  14.9 78.2 %copy-start.23 = (f32[2048]{0:T(1024)}, f32[2048]{0:T(1024)S(1)}, u32[]{:S(2)}) copy-start(f32[2048]{0:T(1024)S(1)} %convert_element_type.133) | copy-start | bytes 24580
  25.4 65.7 %copy-start.10 = (f32[4,256,64]{1,2,0:T(8,128)}, f32[4,256,64]{1,2,0:T(8,128)S(1)}, u32[]{:S(2)}) copy-start(f32[4,256,64]{1,2,0:T(8,128)S(1)} %get-tuple-element.48) | copy-start | bytes 786436
  25.4 65.7 %copy-start.12 = (f32[4,256,64]{1,2,0:T(8,128)}, f32[4,256,64]{1,2,0:T(8,128)S(1)}, u32[]{:S(2)}) copy-start(f32[4,256,64]{1,2,0:T(8,128)S(1)} %get-tuple-element.49) | copy-start | bytes 786436
  84.0 4.7 copy-start.7
  84.0 4.7 copy-start.16
  91.8 59.9 %copy-start.17 = (bf16[4,256,4,64]{1,3,2,0:T(8,128)(2,1)}, bf16[4,256,4,64]{1,3,2,0:T(8,128)(2,1)S(1)}, u32[]{:S(2)}) copy-start(bf16[4,256,4,64]{1,3,2,0:T(8,128)(2,1)S(1)} %get-tuple-element.40) | copy-start | bytes 1572868
  91.8 59.9 %copy-start.19 = (bf16[4,256,4,64]{1,3,2,0:T(8,128)(2,1)}, bf16[4,256,4,64]{1,3,2,0:T(8,128)(2,1)S(1)}, u32[]{:S(2)}) copy-start(bf16[4,256,4,64]{1,3,2,0:T(8,128)(2,1)S(1)} %get-tuple-element.41) | copy-start | bytes 1572868
  93.0 95.2 %all-gather.12.cloned.1.call-start = ((), (), s32[]{:S(2)}) async-start(), calls=%async_computation.10 | async-start | bytes 5242880 | tf_op jit(solution)/shard_map/all_gather | solution.py:127
  93.1 27.8 %copy-start.25 = (f32[1,2,4,128]{3,1,2,0:T(2,128)}, f32[1,2,4,128]{3,1,2,0:T(2,128)S(1)}, u32[]{:S(2)}) copy-start(f32[1,2,4,128]{3,1,2,0:T(2,128)S(1)} %copy.68) | copy-start | bytes 12292
  98.3 23.2 copy-start.28
  120.9 101.8 %all-gather.20.cloned.1.call-start = ((), (), s32[]{:S(2)}) async-start(), calls=%async_computation.14 | async-start | bytes 3145728 | tf_op jit(solution)/shard_map/all_gather | solution.py:91
  121.5 399.4 %all-reduce.8.cloned.1.call-start = ((), (), s32[]{:S(2)}) async-start(), calls=%async_computation.15 | async-start | bytes 16777216 | tf_op jit(solution)/shard_map/psum | solution.py:136
  127.6 66.8 %copy-start.4 = (pred[4,256,1024]{2,1,0:T(8,128)(4,1)}, pred[4,256,1024]{2,1,0:T(8,128)(4,1)S(1)}, u32[]{:S(2)}) copy-start(pred[4,256,1024]{2,1,0:T(8,128)(4,1)S(1)} %broadcast_compare_fusion) | copy-start | bytes 3145732
  206.1 23.8 copy-start.8
  230.0 2.1 copy-start.29
  230.0 395.5 %all-gather.22.cloned.1.call-start = ((), (), s32[]{:S(2)}) async-start(), calls=%async_computation.16 | async-start | bytes 12582912 | tf_op jit(solution)/shard_map/all_gather | solution.py:139
  230.7 500.3 %all-gather.24.cloned.1.call-start = ((), (), s32[]{:S(2)}) async-start(), calls=%async_computation.17 | async-start | bytes 12582912 | tf_op jit(solution)/shard_map/all_gather | solution.py:140
  231.5 605.0 %all-gather.26.cloned.1.call-start = ((), (), s32[]{:S(2)}) async-start(), calls=%async_computation.18 | async-start | bytes 12582912 | tf_op jit(solution)/shard_map/all_gather | solution.py:141
  232.0 1227.5 %all-reduce.12.cloned.1.call-start = ((), (), s32[]{:S(2)}) async-start(), calls=%async_computation.29 | async-start | bytes 33554432 | tf_op jit(solution)/shard_map/psum | solution.py:152
  528.5 4.3 copy-start
  858.3 12.7 copy-start.30
  871.1 12.7 copy-start.32
  897.2 678.3 %reduce-scatter.10.cloned.1.call-start = ((), (), s32[]{:S(2)}) async-start(), calls=%async_computation.19 | async-start | bytes 10485760 | tf_op jit(solution)/shard_map/reduce_scatter | solution.py:214
  1459.5 15.1 copy-start.3
  1459.6 15.1 copy-start.6
  1479.4 3.3 copy-start.1
  1482.6 6.7 copy-start.5
  1489.3 9.5 copy-start.18
  1498.8 6.3 copy-start.2
  1505.2 144.3 %reduce-scatter.12.cloned.1.call-start = ((), (), s32[]{:S(2)}) async-start(), calls=%async_computation.20 | async-start | bytes 10485760 | tf_op jit(solution)/shard_map/reduce_scatter | solution.py:215
  1527.3 48.2 %copy-start.11 = (f32[4,256,64]{1,2,0:T(8,128)S(1)}, f32[4,256,64]{1,2,0:T(8,128)}, u32[]{:S(2)}) copy-start(f32[4,256,64]{1,2,0:T(8,128)} %copy-done.10) | copy-start | bytes 786436
  1527.3 48.2 %copy-start.13 = (f32[4,256,64]{1,2,0:T(8,128)S(1)}, f32[4,256,64]{1,2,0:T(8,128)}, u32[]{:S(2)}) copy-start(f32[4,256,64]{1,2,0:T(8,128)} %copy-done.12) | copy-start | bytes 786436
  1527.3 427.5 %all-reduce.10.cloned.1.call-start = ((), (), s32[]{:S(2)}) async-start(), calls=%async_computation.21 | async-start | bytes 16777216 | tf_op jit(solution)/shard_map/psum | solution.py:228
  1579.3 76.4 %copy-start.15 = (bf16[2048,512]{1,0:T(8,128)(2,1)S(1)}, bf16[2048,512]{1,0:T(8,128)(2,1)}, u32[]{:S(2)}) copy-start(bf16[2048,512]{1,0:T(8,128)(2,1)} %all-gather.14.cloned.1.call-done) | copy-start | bytes 6291460
  1649.5 6.1 copy-start.21
  1655.6 2.4 copy-start.14
  1663.9 1.2 copy-start.9
  1663.9 344.9 %reduce-scatter.20.cloned.1.call-start = ((), (), s32[]{:S(2)}) async-start(), calls=%async_computation.25 | async-start | bytes 4718592 | tf_op jit(solution)/shard_map/reduce_scatter | solution.py:244
  1672.9 456.1 %reduce-scatter.22.cloned.1.call-start = ((), (), s32[]{:S(2)}) async-start(), calls=%async_computation.26 | async-start | bytes 18874368 | tf_op jit(solution)/shard_map/reduce_scatter | solution.py:246
  1688.5 560.7 %reduce-scatter.24.cloned.1.call-start = ((), (), s32[]{:S(2)}) async-start(), calls=%async_computation.27 | async-start | bytes 18874368 | tf_op jit(solution)/shard_map/reduce_scatter | solution.py:247
  1703.9 665.3 %reduce-scatter.26.cloned.1.call-start = ((), (), s32[]{:S(2)}) async-start(), calls=%async_computation.28 | async-start | bytes 18874368 | tf_op jit(solution)/shard_map/reduce_scatter | solution.py:248
  1719.6 6.8 copy-start.22
  1719.6 704.7 %reduce-scatter.18.cloned.1.call-start = ((), (), s32[]{:S(2)}) async-start(), calls=%async_computation.24 | async-start | bytes 4718592 | tf_op jit(solution)/shard_map/reduce_scatter | solution.py:243
  1726.3 753.0 %reduce-scatter.14.cloned.1.call-start = ((), (), s32[]{:S(2)}) async-start(), calls=%async_computation.22 | async-start | bytes 4718592 | tf_op jit(solution)/shard_map/reduce_scatter | solution.py:241
  1726.4 6.7 copy-start.20
  1733.0 6.7 copy-start.31
  1733.1 7.9 copy-start.26
  1733.1 221.8 %copy-start.24 = (f32[2048]{0:T(1024)S(1)}, f32[2048]{0:T(1024)}, u32[]{:S(2)}) copy-start(f32[2048]{0:T(1024)} %copy-done.23) | copy-start | bytes 24580
  1733.1 801.4 %reduce-scatter.16.cloned.1.call-start = ((), (), s32[]{:S(2)}) async-start(), calls=%async_computation.23 | async-start | bytes 4718592 | tf_op jit(solution)/shard_map/reduce_scatter | solution.py:242
  1739.7 221.6 %copy-start.27 = (f32[2048]{0:T(1024)S(1)}, f32[2048]{0:T(1024)}, u32[]{:S(2)}) copy-start(f32[2048]{0:T(1024)} %get-tuple-element.21) | copy-start | bytes 24580
Sparse Core Ops, SparseCore 0:
  9.5 35.8 all-gather.15
  46.9 33.0 all-gather.13
  81.6 33.0 all-gather.9
  116.7 34.9 all-gather.17
  153.7 34.4 all-gather.11
  189.6 33.0 all-gather.19
  230.1 290.8 all-reduce.7
  522.5 102.9 all-gather.21
  627.0 103.9 all-gather.23
  732.4 103.9 all-gather.25
  897.3 562.2 all-reduce.11
  1505.3 70.1 reduce-scatter.9
  1578.1 71.3 reduce-scatter.11
  1664.0 290.8 all-reduce.9
  1958.6 50.0 reduce-scatter.19
  2012.7 116.1 reduce-scatter.21
  2133.0 116.1 reduce-scatter.23
  2253.2 115.9 reduce-scatter.25
  2373.1 51.1 reduce-scatter.17
  2428.1 51.1 reduce-scatter.13
  2483.3 51.1 reduce-scatter.15
where the time goes:
time: 2550 us
  waiting for transfers between devices  2110 us (83%)
  matrix products  260 us (10%)
  other arithmetic  69.3 us (3%)
  blocking collectives  41.2 us (2%)
  local copies, waits for them, and re-layouts  38.8 us (2%)
    psum x1, waiting for transfers between devices, local(): feed_out = lax.psum(plain_dot(hidden, down_full), 'tp')  562 us
    psum x1, waiting for transfers between devices, local(): attend_out = lax.psum(plain_dot(mixed_rows, output_full), 'tp')  284 us
    psum x1, waiting for transfers between devices, local(): lax.psum(dot_last(grad_query_rows, query_full) + dot_last(grad_key_rows,...  214 us
    reduce_scatter x1, waiting for transfers between devices, local(): lax.psum_scatter(grad_gate_w, ('fsdp', 'ctx'), scatter_dimension=0, tiled...  120 us
    reduce_scatter x1, waiting for transfers between devices, local(): lax.psum_scatter(grad_up_w, ('fsdp', 'ctx'), scatter_dimension=0, tiled=T...  120 us
    reduce_scatter x1, waiting for transfers between devices, local(): lax.psum_scatter(grad_down, ('fsdp', 'ctx'), scatter_dimension=1, tiled=T...  120 us
    all_gather x1, waiting for transfers between devices, local(): lax.all_gather(w_up, 'fsdp', axis=0, tiled=True)  91 us
    all_gather x1, waiting for transfers between devices, local(): lax.all_gather(w_down, 'fsdp', axis=1, tiled=True)  90.9 us
  transfers between devices with their start and end apart: 21, of which 21 were waited for; matrix products, arithmetic and copies ran while one was open for 9% of the time, Pallas kernels for 0%

commit v1 on v0

--- a/solution.py
+++ b/solution.py
@@ -7,6 +7,23 @@
 HD = 128
 norm_epsilon = 1e-05
 rope_base = 10000.0
+
+
+def _put_slot(view):
+    group_axis = "fsdp"
+    mid_arr = lax.axis_size(group_axis)
+    t_next = lax.axis_index(group_axis)
+    outcome_arr, opened = (mid_arr, t_next)
+    answer, f_next = (view, 1)
+    while f_next < outcome_arr:
+        plain = lax.ppermute(
+            answer, group_axis, [(nth, nth ^ f_next) for nth in range(outcome_arr)]
+        )
+        part_now = jnp.concatenate([answer, plain], axis=1)
+        local_out = jnp.concatenate([plain, answer], axis=1)
+        answer = jnp.where(opened & f_next == 0, part_now, local_out)
+        f_next = 2 * f_next
+    return answer
 
 
 def plain_dot(left_side, right_side):
@@ -138,7 +155,7 @@
     gate_full, up_full, down_full, gain_two = (
         lax.all_gather(w_gate, "fsdp", axis=0, tiled=True),
         lax.all_gather(w_up, "fsdp", axis=0, tiled=True),
-        lax.all_gather(w_down, "fsdp", axis=1, tiled=True),
+        _put_slot(w_down),
         lax.all_gather(gain_feed, "fsdp", axis=0, tiled=True),
     )
     gain_two = gain_two.astype(jnp.float32)

time: 2550 us -> 2560 us (level)
  blocking collectives: 41.2 us -> 129 us
  waiting for transfers between devices: 2110 us -> 2030 us
    psum x1, waiting for transfers between devices: 284 us -> 196 us  [local(): attend_out = lax.psum(plain_dot(mixed_rows, output_full), 'tp')]
    all_gather x1, blocking collectives: 4.77 us -> 92.2 us  [local(): lax.all_gather(gain_feed, 'fsdp', axis=0, tiled=True)]
  transfers between devices with their start and end apart: 21 -> 22, of which waited for: 21 -> 21; matrix products, arithmetic and copies ran while one was open for 9% -> 11% of each run, Pallas kernels for 0% -> 0%
where the time goes in v1:
time: 2560 us; the launch traced here: 2550 us
  waiting for transfers between devices  2030 us (79%)
  matrix products  265 us (10%)
  blocking collectives  129 us (5%)
  other arithmetic  69.3 us (3%)
  local copies, waits for them, and re-layouts  38.8 us (2%)
    psum x1, waiting for transfers between devices, local(): feed_out = lax.psum(plain_dot(hidden, down_full), 'tp')  562 us
    psum x1, waiting for transfers between devices, local(): lax.psum(dot_last(grad_query_rows, query_full) + dot_last(grad_key_rows,...  214 us
    psum x1, waiting for transfers between devices, local(): attend_out = lax.psum(plain_dot(mixed_rows, output_full), 'tp')  196 us
    reduce_scatter x1, waiting for transfers between devices, local(): lax.psum_scatter(grad_gate_w, ('fsdp', 'ctx'), scatter_dimension=0, tiled...  120 us
    reduce_scatter x1, waiting for transfers between devices, local(): lax.psum_scatter(grad_up_w, ('fsdp', 'ctx'), scatter_dimension=0, tiled=T...  120 us
    reduce_scatter x1, waiting for transfers between devices, local(): lax.psum_scatter(grad_down, ('fsdp', 'ctx'), scatter_dimension=1, tiled=T...  120 us
    all_gather x1, blocking collectives, local(): lax.all_gather(gain_feed, 'fsdp', axis=0, tiled=True)  92.2 us
    all_gather x1, waiting for transfers between devices, local(): lax.all_gather(w_up, 'fsdp', axis=0, tiled=True)  91.1 us
  transfers between devices with their start and end apart: 22, of which 21 were waited for; matrix products, arithmetic and copies ran while one was open for 11% of the time, Pallas kernels for 0%

profile of v1, /device:TPU:0, one launch (start us, length us, event | category | flops | bytes accessed | tf_op | source)
XLA Modules:
  0.0 2551.0 jit_solution(15852639095356110210)
XLA Ops:
  9.4 5.5 all_gather.45
  14.9 3.1 fusion.10
  18.7 5.6 fusion.12
  25.4 20.0 all-gather.16.cloned.1.call-done
  45.4 2.9 copy.52
  48.3 31.7 %all-gather.14.cloned.1.call-done = bf16[2048,512]{1,0:T(8,128)(2,1)} async-done(((bf16[1024,512]{1,0:T(8,128)(2,1)}), bf16[2048,512]{1,0:T(8,128)(2,1)}) %all-gather.14.cloned.1.call-update) | async-done | bytes 2097168 | tf_op jit(solution)/shard_map/all_gather | solution.py:105
  80.0 3.9 copy.51
  84.0 4.7 fusion.20
  93.1 5.2 fusion.8
  98.3 16.4 all-gather.10.cloned.1.call-done
  114.7 6.2 convolution_convert_fusion
  121.6 5.4 all_gather.48
  127.6 24.1 all-gather.18.cloned.1.call-done
  151.7 11.6 add_divide_fusion
  163.3 24.9 all-gather.12.cloned.1.call-done
  188.2 6.2 copy.50
  194.4 11.0 fusion.34
  206.1 16.6 all-gather.20.cloned.1.call-done
  222.7 7.2 fusion.44
  232.5 92.2 %all_gather.53 = bf16[2048]{0:T(1024)(128)(2,1)S(1)} all-gather(bf16[1024]{0:T(1024)(128)(2,1)S(1)} %copy-done.30), channel_id=1, replica_groups=mesh['fsdp'=2,'ctx'=4,'tp'=4] {'fsdp'}, dimensions={0}, use_global_device_ids=true | all-gather | bytes 6144 | tf_op jit(solution)/shard_map/all_gather | solution.py:159
  324.7 196.3 %all-reduce.8.cloned.1.call-done = f32[1024,2048]{1,0:T(8,128)} async-done(((f32[1024,2048]{1,0:T(8,128)}), f32[1024,2048]{1,0:T(8,128)}) %all-reduce.8.cloned.1.call-update) | async-done | bytes 8388624 | tf_op jit(solution)/shard_map/psum | solution.py:153
  520.9 7.6 multiply_reduce_fusion.5
  528.5 4.3 copy-done
  535.5 89.9 %all-gather.22.cloned.1.call-done = bf16[2048,2048]{1,0:T(8,128)(2,1)} async-done(((bf16[1024,2048]{1,0:T(8,128)(2,1)}), bf16[2048,2048]{1,0:T(8,128)(2,1)}) %all-gather.22.cloned.1.call-update) | async-done | bytes 8388624 | tf_op jit(solution)/shard_map/all_gather | solution.py:156
  625.5 14.4 fusion.59
  639.9 91.1 %all-gather.24.cloned.1.call-done = bf16[2048,2048]{1,0:T(8,128)(2,1)} async-done(((bf16[1024,2048]{1,0:T(8,128)(2,1)}), bf16[2048,2048]{1,0:T(8,128)(2,1)}) %all-gather.24.cloned.1.call-update) | async-done | bytes 8388624 | tf_op jit(solution)/shard_map/all_gather | solution.py:157
  731.0 14.4 fusion.60
  745.5 91.0 %all-gather.26.cloned.1.call-done = bf16[2048,2048]{1,0:T(8,128)(2,1)} async-done(((bf16[2048,1024]{1,0:T(8,128)(2,1)}), bf16[2048,2048]{1,0:T(8,128)(2,1)}) %all-gather.26.cloned.1.call-update) | async-done | bytes 8388624 | tf_op jit(solution)/shard_map/all_gather | solution.py:187
  836.4 21.9 multiply_convert_fusion
  858.3 14.6 fusion.61
  873.0 14.9 convolution_add_fusion
  887.8 15.1 fusion
  903.0 562.3 %all-reduce.12.cloned.1.call-done = (f32[1024,2048]{1,0:T(8,128)}, f32[1024,2048]{1,0:T(8,128)}) async-done(((f32[1024,2048]{1,0:T(8,128)}, f32[1024,2048]{1,0:T(8,128)}), (f32[1024,2048]{1,0:T(8,128)}, f32[1024,2048]{1,0:T(8,128)})) %all-reduce.12.cloned.1.call-update) | async-done | bytes 16777232 | tf_op jit(solution)/shard_map/psum | solution.py:169
  1465.3 15.1 multiply_reduce_fusion
  1480.4 4.7 subtract_add_fusion
  1485.2 3.2 copy-done.1
  1488.4 4.0 fusion.30
  1495.1 9.5 select_convert_fusion
  1504.6 6.3 broadcast_multiply_fusion
  1511.0 13.1 fusion.24
  1524.1 9.0 copy.61
  1533.2 7.7 multiply_bitcast_fusion
  1540.9 40.4 %reduce-scatter.10.cloned.1.call-done = f32[4,256,512]{1,2,0:T(8,128)} async-done(((f32[4,1024,512]{1,2,0:T(8,128)}), f32[4,256,512]{1,2,0:T(8,128)}) %reduce-scatter.10.cloned.1.call-update) | async-done | bytes 2097168 | tf_op jit(solution)/shard_map/reduce_scatter | solution.py:231
  1586.4 68.9 %reduce-scatter.12.cloned.1.call-done = f32[4,256,512]{2,1,0:T(8,128)} async-done(((f32[4,1024,512]{2,1,0:T(8,128)}), f32[4,256,512]{2,1,0:T(8,128)}) %reduce-scatter.12.cloned.1.call-update) | async-done | bytes 2097168 | tf_op jit(solution)/shard_map/reduce_scatter | solution.py:232
  1657.1 4.3 fusion.37
  1663.8 5.8 add_add_fusion
  1670.9 7.7 fusion.26
  1678.7 15.4 fusion.62
  1694.2 15.2 fusion.63
  1709.5 15.5 fusion.64
  1725.1 6.6 convolution_bitcast_fusion
  1731.8 6.6 fusion.39
  1738.5 6.5 fusion.35
  1746.3 214.3 %all-reduce.10.cloned.1.call-done = f32[1024,2048]{1,0:T(8,128)} async-done(((f32[1024,2048]{1,0:T(8,128)}), f32[1024,2048]{1,0:T(8,128)}) %all-reduce.10.cloned.1.call-update) | async-done | bytes 8388624 | tf_op jit(solution)/shard_map/psum | solution.py:245
  1960.7 6.4 fusion.9
  1967.1 25.5 %all-reduce.2 = (f32[2048]{0:T(1024)S(1)}, f32[2048]{0:T(1024)S(1)}, f32[]{:T(128)}, f32[]{:T(128)}, f32[]{:T(128)}) all-reduce(f32[2048]{0:T(1024)S(1)} %get-tuple-element.16, f32[2048]{0:T(1024)S(1)} %copy-done.28, f32[]{:T(128)} %get-tuple-element.19, ...), channel_id=4, replica_groups=mesh['fsdp'=2,'ctx'=4,'tp'=4] {'fsdp','ctx'}, use_global_device_ids=true, to_apply=%region_11.12.clone | all-reduce | flops 4099 | bytes 32792
  1996.0 10.5 fusion.16
  2006.5 8.1 reduce-scatter.20.cloned.1.call-done
  2014.6 120.2 %reduce-scatter.22.cloned.1.call-done = f32[256,2048]{1,0:T(8,128)} async-done(((f32[2048,2048]{1,0:T(8,128)}), f32[256,2048]{1,0:T(8,128)}) %reduce-scatter.22.cloned.1.call-update) | async-done | bytes 2097168 | tf_op jit(solution)/shard_map/reduce_scatter | solution.py:263
  2134.8 120.2 %reduce-scatter.24.cloned.1.call-done = f32[256,2048]{1,0:T(8,128)} async-done(((f32[2048,2048]{1,0:T(8,128)}), f32[256,2048]{1,0:T(8,128)}) %reduce-scatter.24.cloned.1.call-update) | async-done | bytes 2097168 | tf_op jit(solution)/shard_map/reduce_scatter | solution.py:264
  2255.0 120.0 %reduce-scatter.26.cloned.1.call-done = f32[2048,256]{1,0:T(8,128)} async-done(((f32[2048,2048]{1,0:T(8,128)}), f32[2048,256]{1,0:T(8,128)}) %reduce-scatter.26.cloned.1.call-update) | async-done | bytes 2097168 | tf_op jit(solution)/shard_map/reduce_scatter | solution.py:265
  2375.0 55.1 %reduce-scatter.18.cloned.1.call-done = f32[256,512]{1,0:T(8,128)} async-done(((f32[2048,512]{1,0:T(8,128)}), f32[256,512]{1,0:T(8,128)}) %reduce-scatter.18.cloned.1.call-update) | async-done | bytes 524304 | tf_op jit(solution)/shard_map/reduce_scatter | solution.py:260
  2430.1 55.0 %reduce-scatter.14.cloned.1.call-done = f32[256,512]{1,0:T(8,128)} async-done(((f32[2048,512]{1,0:T(8,128)}), f32[256,512]{1,0:T(8,128)}) %reduce-scatter.14.cloned.1.call-update) | async-done | bytes 524304 | tf_op jit(solution)/shard_map/reduce_scatter | solution.py:258
  2485.1 55.1 %reduce-scatter.16.cloned.1.call-done = f32[256,512]{1,0:T(8,128)} async-done(((f32[2048,512]{1,0:T(8,128)}), f32[256,512]{1,0:T(8,128)}) %reduce-scatter.16.cloned.1.call-update) | async-done | bytes 524304 | tf_op jit(solution)/shard_map/reduce_scatter | solution.py:259
  (138 shorter events, 31.1 us)
Async XLA Ops:
  7.2 38.2 %all-gather.16.cloned.1.call-start = ((), (), s32[]{:S(2)}) async-start(), calls=%async_computation.12 | async-start | bytes 3145728 | tf_op jit(solution)/shard_map/all_gather | solution.py:106
  7.9 72.1 %all-gather.14.cloned.1.call-start = ((), (), s32[]{:S(2)}) async-start(), calls=%async_computation.11 | async-start | bytes 3145728 | tf_op jit(solution)/shard_map/all_gather | solution.py:105
  8.7 106.1 %all-gather.10.cloned.1.call-start = ((), (), s32[]{:S(2)}) async-start(), calls=%async_computation.9 | async-start | bytes 3145728 | tf_op jit(solution)/shard_map/all_gather | solution.py:107
  9.4 142.3 %all-gather.18.cloned.1.call-start = ((), (), s32[]{:S(2)}) async-start(), calls=%async_computation.13 | async-start | bytes 5242880 | tf_op jit(solution)/shard_map/all_gather | solution.py:143
  14.9 78.2 %copy-start.24 = (f32[2048]{0:T(1024)}, f32[2048]{0:T(1024)S(1)}, u32[]{:S(2)}) copy-start(f32[2048]{0:T(1024)S(1)} %convert_element_type.133) | copy-start | bytes 24580
  25.4 65.7 %copy-start.11 = (f32[4,256,64]{1,2,0:T(8,128)}, f32[4,256,64]{1,2,0:T(8,128)S(1)}, u32[]{:S(2)}) copy-start(f32[4,256,64]{1,2,0:T(8,128)S(1)} %get-tuple-element.48) | copy-start | bytes 786436
  25.4 65.7 %copy-start.13 = (f32[4,256,64]{1,2,0:T(8,128)}, f32[4,256,64]{1,2,0:T(8,128)S(1)}, u32[]{:S(2)}) copy-start(f32[4,256,64]{1,2,0:T(8,128)S(1)} %get-tuple-element.49) | copy-start | bytes 786436
  84.0 4.7 copy-start.8
  84.0 4.7 copy-start.17
  91.8 59.9 %copy-start.18 = (bf16[4,256,4,64]{1,3,2,0:T(8,128)(2,1)}, bf16[4,256,4,64]{1,3,2,0:T(8,128)(2,1)S(1)}, u32[]{:S(2)}) copy-start(bf16[4,256,4,64]{1,3,2,0:T(8,128)(2,1)S(1)} %get-tuple-element.40) | copy-start | bytes 1572868
  91.8 59.9 %copy-start.20 = (bf16[4,256,4,64]{1,3,2,0:T(8,128)(2,1)}, bf16[4,256,4,64]{1,3,2,0:T(8,128)(2,1)S(1)}, u32[]{:S(2)}) copy-start(bf16[4,256,4,64]{1,3,2,0:T(8,128)(2,1)S(1)} %get-tuple-element.41) | copy-start | bytes 1572868
  93.0 95.2 %all-gather.12.cloned.1.call-start = ((), (), s32[]{:S(2)}) async-start(), calls=%async_computation.10 | async-start | bytes 5242880 | tf_op jit(solution)/shard_map/all_gather | solution.py:144
  93.1 27.8 %copy-start.26 = (f32[1,2,4,128]{3,1,2,0:T(2,128)}, f32[1,2,4,128]{3,1,2,0:T(2,128)S(1)}, u32[]{:S(2)}) copy-start(f32[1,2,4,128]{3,1,2,0:T(2,128)S(1)} %copy.68) | copy-start | bytes 12292
  98.3 23.2 copy-start.29
  120.9 101.8 %all-gather.20.cloned.1.call-start = ((), (), s32[]{:S(2)}) async-start(), calls=%async_computation.14 | async-start | bytes 3145728 | tf_op jit(solution)/shard_map/all_gather | solution.py:108
  121.5 399.4 %all-reduce.8.cloned.1.call-start = ((), (), s32[]{:S(2)}) async-start(), calls=%async_computation.15 | async-start | bytes 16777216 | tf_op jit(solution)/shard_map/psum | solution.py:153
  127.6 66.8 %copy-start.4 = (pred[4,256,1024]{2,1,0:T(8,128)(4,1)}, pred[4,256,1024]{2,1,0:T(8,128)(4,1)S(1)}, u32[]{:S(2)}) copy-start(pred[4,256,1024]{2,1,0:T(8,128)(4,1)S(1)} %broadcast_compare_fusion) | copy-start | bytes 3145732
  206.1 23.8 copy-start.9
  230.0 2.5 copy-start.30
  230.0 395.5 %all-gather.22.cloned.1.call-start = ((), (), s32[]{:S(2)}) async-start(), calls=%async_computation.16 | async-start | bytes 12582912 | tf_op jit(solution)/shard_map/all_gather | solution.py:156
  230.7 500.3 %all-gather.24.cloned.1.call-start = ((), (), s32[]{:S(2)}) async-start(), calls=%async_computation.17 | async-start | bytes 12582912 | tf_op jit(solution)/shard_map/all_gather | solution.py:157
  231.5 605.0 %all-gather.26.cloned.1.call-start = ((), (), s32[]{:S(2)}) async-start(), calls=%async_computation.18 | async-start | bytes 12582912 | tf_op jit(solution)/shard_map/all_gather | solution.py:187
  232.0 1233.3 %all-reduce.12.cloned.1.call-start = ((), (), s32[]{:S(2)}) async-start(), calls=%async_computation.29 | async-start | bytes 33554432 | tf_op jit(solution)/shard_map/psum | solution.py:169
  232.1 655.7 %collective-permute-start = (bf16[2048,1024]{1,0:T(8,128)(2,1)}, bf16[2048,1024]{1,0:T(8,128)(2,1)}, u32[]{:S(2)}, u32[]{:S(2)}) collective-permute-start(bf16[2048,1024]{1,0:T(8,128)(2,1)} %param.24), channel_id=1, source_target_pairs={{0,16},{16,0},{1,17},{17,1},{2,18},{18,2},{3,19},{19,3},{4,20},{20... | collective-permute-start | bytes 12582920 | tf_op jit(solution)/shard_map/ppermute | solution.py:19
  528.5 4.3 copy-start
  858.3 14.6 copy-start.32
  873.0 14.9 copy-start.7
  902.9 678.4 %reduce-scatter.10.cloned.1.call-start = ((), (), s32[]{:S(2)}) async-start(), calls=%async_computation.19 | async-start | bytes 10485760 | tf_op jit(solution)/shard_map/reduce_scatter | solution.py:231
  1465.3 15.1 copy-start.3
  1465.3 15.1 copy-start.6
  1485.1 3.3 copy-start.1
  1488.4 6.7 copy-start.5
  1495.1 9.5 copy-start.19
  1504.6 6.3 copy-start.2
  1511.0 144.3 %reduce-scatter.12.cloned.1.call-start = ((), (), s32[]{:S(2)}) async-start(), calls=%async_computation.20 | async-start | bytes 10485760 | tf_op jit(solution)/shard_map/reduce_scatter | solution.py:232
  1533.1 48.2 %copy-start.12 = (f32[4,256,64]{1,2,0:T(8,128)S(1)}, f32[4,256,64]{1,2,0:T(8,128)}, u32[]{:S(2)}) copy-start(f32[4,256,64]{1,2,0:T(8,128)} %copy-done.11) | copy-start | bytes 786436
  1533.1 48.2 %copy-start.14 = (f32[4,256,64]{1,2,0:T(8,128)S(1)}, f32[4,256,64]{1,2,0:T(8,128)}, u32[]{:S(2)}) copy-start(f32[4,256,64]{1,2,0:T(8,128)} %copy-done.13) | copy-start | bytes 786436
  1533.1 427.6 %all-reduce.10.cloned.1.call-start = ((), (), s32[]{:S(2)}) async-start(), calls=%async_computation.21 | async-start | bytes 16777216 | tf_op jit(solution)/shard_map/psum | solution.py:245
  1585.0 76.4 %copy-start.16 = (bf16[2048,512]{1,0:T(8,128)(2,1)S(1)}, bf16[2048,512]{1,0:T(8,128)(2,1)}, u32[]{:S(2)}) copy-start(bf16[2048,512]{1,0:T(8,128)(2,1)} %all-gather.14.cloned.1.call-done) | copy-start | bytes 6291460
  1655.3 6.1 copy-start.22
  1661.4 2.4 copy-start.15
  1669.7 1.2 copy-start.10
  1669.7 344.9 %reduce-scatter.20.cloned.1.call-start = ((), (), s32[]{:S(2)}) async-start(), calls=%async_computation.25 | async-start | bytes 4718592 | tf_op jit(solution)/shard_map/reduce_scatter | solution.py:261
  1678.7 456.1 %reduce-scatter.22.cloned.1.call-start = ((), (), s32[]{:S(2)}) async-start(), calls=%async_computation.26 | async-start | bytes 18874368 | tf_op jit(solution)/shard_map/reduce_scatter | solution.py:263
  1694.1 560.8 %reduce-scatter.24.cloned.1.call-start = ((), (), s32[]{:S(2)}) async-start(), calls=%async_computation.27 | async-start | bytes 18874368 | tf_op jit(solution)/shard_map/reduce_scatter | solution.py:264
  1709.4 665.6 %reduce-scatter.26.cloned.1.call-start = ((), (), s32[]{:S(2)}) async-start(), calls=%async_computation.28 | async-start | bytes 18874368 | tf_op jit(solution)/shard_map/reduce_scatter | solution.py:265
  1725.0 6.8 copy-start.23
  1725.0 705.1 %reduce-scatter.18.cloned.1.call-start = ((), (), s32[]{:S(2)}) async-start(), calls=%async_computation.24 | async-start | bytes 4718592 | tf_op jit(solution)/shard_map/reduce_scatter | solution.py:260
  1731.7 753.4 %reduce-scatter.14.cloned.1.call-start = ((), (), s32[]{:S(2)}) async-start(), calls=%async_computation.22 | async-start | bytes 4718592 | tf_op jit(solution)/shard_map/reduce_scatter | solution.py:258
  1731.8 6.7 copy-start.21
  1738.4 6.7 copy-start.31
  1738.4 7.9 copy-start.27
  1738.4 222.2 %copy-start.25 = (f32[2048]{0:T(1024)S(1)}, f32[2048]{0:T(1024)}, u32[]{:S(2)}) copy-start(f32[2048]{0:T(1024)} %copy-done.24) | copy-start | bytes 24580
  1738.4 801.8 %reduce-scatter.16.cloned.1.call-start = ((), (), s32[]{:S(2)}) async-start(), calls=%async_computation.23 | async-start | bytes 4718592 | tf_op jit(solution)/shard_map/reduce_scatter | solution.py:259
  1745.0 222.0 %copy-start.28 = (f32[2048]{0:T(1024)S(1)}, f32[2048]{0:T(1024)}, u32[]{:S(2)}) copy-start(f32[2048]{0:T(1024)} %get-tuple-element.21) | copy-start | bytes 24580
Sparse Core Ops, SparseCore 0:
  9.5 35.8 all-gather.15
  46.9 33.0 all-gather.13
  81.6 33.0 all-gather.9
  116.7 34.9 all-gather.17
  153.7 34.4 all-gather.11
  189.6 33.0 all-gather.19
  230.1 290.8 all-reduce.7
  522.5 102.9 all-gather.21
  627.0 103.9 all-gather.23
  732.4 103.9 all-gather.25
  903.0 562.2 all-reduce.11
  1511.1 70.1 reduce-scatter.9
  1583.8 71.3 reduce-scatter.11
  1669.8 290.8 all-reduce.9
  1964.5 50.0 reduce-scatter.19
  2018.6 116.1 reduce-scatter.21
  2138.8 116.1 reduce-scatter.23
  2259.0 115.9 reduce-scatter.25
  2378.9 51.1 reduce-scatter.17
  2433.9 51.1 reduce-scatter.13
  2489.1 51.1 reduce-scatter.15
